TPU v7x, 256 devices: a 8x8x2 block of a 8x8x16 slice. The times are simulated.
256 devices in a mesh: grp: 2 (over z), kvp: 16 (over x, core), tp: 8 (over y).
Axes of the slice: x: 8, y: 8, z: 2, core: 2. Of those that a mesh axis runs over, the one named last changes fastest.
The devices are a block of a 8x8x16 slice.
Arguments:
- hidden_in: bfloat16 [16, 7168], P('grp'), parts along dimension 0, may hold values from -3 to 3
- queries_nope: bfloat16 [16, 128, 128], P('grp', ('kvp', 'tp')), parts along dimension 0, may hold values from -6 to 6
- queries_rope: bfloat16 [16, 128, 64], P('grp', ('kvp', 'tp')), parts along dimension 0, may hold values from -26 to 26
- cache: bfloat16 [16, 6144, 576], P('grp', 'kvp'), parts along dimension 0, may hold values from -20 to 20
- lengths: int32 [16], P('grp'), parts along dimension 0, may hold values from 128 to 6144, as said below
- w_uk: bfloat16 [128, 128, 512], P(('kvp', 'tp')), may hold values from -0.5 to 0.5
- w_uv: bfloat16 [128, 512, 128], P(('kvp', 'tp')), may hold values from -0.25 to 0.25
- w_out: bfloat16 [16384, 7168], P(('kvp', 'tp')), may hold values from -0.1875 to 0.1875
- norm_gain: float32 [7168], replicated, may hold values from 0.25 to 1.75
- w_gate: bfloat16 [7168, 18432], P(None, ('kvp', 'tp')), may hold values from -0.0625 to 0.0625
- w_up: bfloat16 [7168, 18432], P(None, ('kvp', 'tp')), may hold values from -0.0625 to 0.0625
- w_down: bfloat16 [18432, 7168], P(('kvp', 'tp')), may hold values from -0.15625 to 0.15625
Outputs:
- layer_out: bfloat16 [16, 7168], P('grp', ('kvp', 'tp')), parts along dimension 0
There are 2 independent parts, one for each index of `grp`. A program takes and returns all parts, laid end to end along the dimension named above; an argument that names none is the same for every part. Nothing has to cross between parts.
Inputs may be any that keep to these rules, and one draw needn't show every extreme that they name: `lengths`: every length is a multiple of 128; in every draw some request has the full 6144.
All inputs are finite; a program needn't handle non-finite values.
Results may differ from a plain program's by a relative error of at most 0.04.
Values may be sent and summed in bfloat16 or wider, within the bound.
A program may use at most 64 MiB of HBM per device.

v0:
```python
import jax
import jax.numpy as jnp
from jax import lax
from jax.sharding import Mesh
from jax.sharding import PartitionSpec as P

KVP = ("kvp_0", "kvp_1")
KVP_TP = ("kvp_0", "kvp_1", "tp")


def in_one_piece(arrays, axis, dim, along):
    both = jnp.concatenate(arrays, axis=along)
    whole, at, gathered = (lax.all_gather(both, axis, axis=dim, tiled=True), 0, [])
    for a in arrays:
        gathered.append(lax.slice_in_dim(whole, at, at + a.shape[along], axis=along))
        at += a.shape[along]
    return tuple(gathered)


def sum_in_order(blocks, axes, sequence):
    inside = blocks.shape[1:]
    blocks = blocks.reshape(*(lax.axis_size(a) for a in axes), *inside)
    blocks = jnp.moveaxis(blocks, sequence, range(len(axes))).reshape(-1, *inside)
    for k in sequence:
        blocks = lax.psum_scatter(blocks, axes[k], scatter_dimension=0, tiled=True)
    return blocks[0]


def in_blocks(value, dim, size):
    dims = value.shape
    blocks = value.reshape(*dims[:dim], size, dims[dim] // size, *dims[dim + 1 :])
    return jnp.moveaxis(blocks, dim, 0)


def sum_by_axis(value, axes, sequence, dim):
    size = lax.axis_size(axes)
    return sum_in_order(in_blocks(value, dim, size), axes, sequence)


def project(o_lat, w_uv, w_out):
    head_out = jnp.einsum("bhl,hle->bhe", o_lat, w_uv, preferred_element_type=jnp.float32).astype(
        jnp.bfloat16
    )
    return jnp.dot(
        head_out.reshape(head_out.shape[0], -1), w_out, preferred_element_type=jnp.float32
    )


def per_device(
    hidden_in,
    queries_nope,
    queries_rope,
    cache,
    lengths,
    w_uk,
    w_uv,
    w_out,
    norm_gain,
    w_gate,
    w_up,
    w_down,
):
    batch, heads_dev, head_dim = queries_nope.shape
    latent = w_uk.shape[2]
    ctx_dev = cache.shape[1]
    groups = lax.axis_size(KVP)
    score_scale = float(head_dim + queries_rope.shape[2]) ** (-0.5)
    q_lat = jnp.einsum(
        "bhd,hdl->bhl", queries_nope, w_uk, preferred_element_type=jnp.float32
    ).astype(jnp.bfloat16)
    q_lat_all, rope_all = in_one_piece((q_lat, queries_rope), KVP, 1, 2)
    q_full = jnp.concatenate([q_lat_all, rope_all], axis=2)
    scores = (
        jnp.einsum("bhc,btc->bht", q_full, cache, preferred_element_type=jnp.float32) * score_scale
    )
    offset = lax.axis_index(KVP) * ctx_dev
    visible = ((offset + jnp.arange(ctx_dev, dtype=jnp.int32))[None, :] < lengths[:, None])[
        :, None, :
    ]
    masked = jnp.where(visible, scores, jnp.float32(-1e30))
    block_max = jnp.max(masked, axis=2)
    exponent = jnp.where(visible, jnp.exp(masked - block_max[..., None]), jnp.float32(0.0))
    guarded = jnp.maximum(jnp.sum(exponent, axis=2), 1.0)
    log_total = block_max + jnp.log(guarded)
    weights = (exponent / guarded[..., None]).astype(jnp.bfloat16)
    partial_value = jnp.einsum("bht,btc->bhc", weights, cache, preferred_element_type=jnp.float32)[
        ..., :latent
    ]
    blocks = partial_value.reshape(batch, groups, heads_dev, latent)
    block_logs = log_total.reshape(batch, groups, heads_dev)
    part_blocks = lax.all_to_all(
        blocks.astype(jnp.bfloat16), KVP, split_axis=1, concat_axis=1, tiled=True
    ).astype(blocks.dtype)
    part_logs = lax.all_to_all(
        block_logs.astype(jnp.bfloat16), KVP, split_axis=1, concat_axis=1, tiled=True
    ).astype(block_logs.dtype)
    highest = jnp.max(part_logs, axis=1)
    overall = highest + jnp.log(jnp.sum(jnp.exp(part_logs - highest[:, None, :]), axis=1))
    scaled = jnp.exp(part_logs - overall[:, None, :])[..., None] * part_blocks
    o_lat = jnp.sum(scaled, axis=1).astype(jnp.bfloat16)
    attention = project(o_lat, w_uv, w_out)
    model_width = norm_gain.shape[0]
    share_width = model_width // lax.axis_size(KVP_TP)
    share_start = lax.axis_index(KVP_TP) * share_width
    attn_whole = lax.psum(attention, KVP_TP)
    residual = hidden_in.astype(jnp.float32) + attn_whole
    mean_square = jnp.mean(residual * residual, axis=1)
    normed = (residual * lax.rsqrt(mean_square + 1e-06)[:, None] * norm_gain[None, :]).astype(
        jnp.bfloat16
    )
    residual_share = lax.dynamic_slice_in_dim(residual, share_start, share_width, 1)
    gate_proj = jnp.dot(normed, w_gate, preferred_element_type=jnp.float32)
    up_proj = jnp.dot(normed, w_up, preferred_element_type=jnp.float32)
    act = (jax.nn.silu(gate_proj) * up_proj).astype(jnp.bfloat16)
    ffn_terms = jnp.dot(act, w_down, preferred_element_type=jnp.float32)
    ffn_share = sum_by_axis(ffn_terms, KVP_TP, (1, 0, 2), 1)
    return (residual_share + ffn_share).astype(jnp.bfloat16)


def solution(mesh):
    torus = Mesh(
        mesh.devices.reshape(mesh.shape["grp"], 8, 2, mesh.shape["tp"]),
        ("grp", "kvp_0", "kvp_1", "tp"),
    )
    return jax.shard_map(
        per_device,
        mesh=torus,
        in_specs=(
            P("grp", None),
            P("grp", KVP_TP, None),
            P("grp", KVP_TP, None),
            P("grp", KVP, None),
            P("grp"),
            P(KVP_TP, None, None),
            P(KVP_TP, None, None),
            P(KVP_TP, None),
            P(),
            P(None, KVP_TP),
            P(None, KVP_TP),
            P(KVP_TP, None),
        ),
        out_specs=P("grp", KVP_TP),
        check_vma=False,
    )
```

profile of v0, /device:TPU:514, one launch (start us, length us, event | category | flops | bytes accessed | tf_op | source)
XLA Modules:
  0.0 365.7 jit_solution(1368219524394948218)
XLA Ops:
  6.6 1.2 fusion.1
  7.7 0.7 pad_maximum_fusion
  8.4 34.0 %all_gather.3 = bf16[8,16,576]{2,0,1:T(8,128)(2,1)S(1)} all-gather(bf16[8,1,576]{2,0,1:T(8,128)(2,1)S(1)} %pad_maximum_fusion), channel_id=1, replica_groups=mesh['grp'=2,'kvp_0'=8,'kvp_1'=2,'tp'=8] {'kvp_0','kvp_1'}, dimensions={1}, use_global_device_ids=true | all-gather | bytes 156672 | tf_op jit(solution)/shard_map/all_gather | solution.py:13
  42.4 0.7 broadcast_compare_fusion
  45.9 3.6 all-to-all-start
  49.5 2.0 fusion.11
  51.6 0.7 copy.27
  52.3 3.4 all-to-all-done
  55.7 5.4 %all-to-all-start.1 = ((bf16[8,16,1,512]{3,0,2,1:T(8,128)(2,1)}), bf16[8,16,1,512]{3,0,2,1:T(8,128)(2,1)}, u32[]{:S(2)}, u32[]{:S(2)}) async-start(bf16[8,16,1,512]{3,0,2,1:T(8,128)(2,1)} %copy.27), calls=%async_computation.1 | async-start | bytes 262144 | tf_op jit(solution)/shard_map/all_to_all | solution.py:91
  61.8 0.8 fusion.24
  62.8 5.9 %all-to-all-done.1 = bf16[8,16,1,512]{3,0,2,1:T(8,128)(2,1)} async-done(((bf16[8,16,1,512]{3,0,2,1:T(8,128)(2,1)}), bf16[8,16,1,512]{3,0,2,1:T(8,128)(2,1)}, u32[]{:S(2)}, u32[]{:S(2)}) %all-to-all-start.1) | async-done | bytes 131104 | tf_op jit(solution)/shard_map/all_to_all | solution.py:91
  68.7 1.0 multiply_reduce_fusion
  69.7 2.7 fusion.4
  72.5 185.7 %all-reduce.3.cloned.1.call-done = f32[8,7168]{1,0:T(8,128)} async-done(((f32[8,7168]{1,0:T(8,128)}), f32[8,7168]{1,0:T(8,128)}) %all-reduce.3.cloned.1.call-update) | async-done | bytes 229392 | tf_op jit(solution)/shard_map/psum | solution.py:105
  258.3 1.2 multiply_reduce_fusion.1
  259.5 0.7 copy-done.1
  260.2 2.3 fusion.34
  262.4 4.6 %fusion.3 = f32[8,7168]{1,0:T(8,128)} fusion(bf16[144,7168]{1,0:T(8,128)(2,1)} %param.23, bf16[7168,144]{0,1:T(8,128)(2,1)} %param.22, f32[8,144]{1,0:T(8,128)S(1)} %fusion.34, f32[8,7168]{1,0:T(8,128)} %copy-done.1, f32[7168]{0:T(1024)} %param.20, f32[8]{0:T(128)S(1)} %add_rsqrt_fusion), kind=kOutput, calls=%fused_computation.6 | convolution fusion | flops 33209088 | bytes 4620832 | tf_op jit(solution)/shard_map/dot_general | solution.py:115
  267.1 2.2 reshape.125
  269.3 2.2 copy.29
  271.5 12.6 %reduce-scatter.3.cloned.1.call-done = f32[64,8,56]{2,1,0:T(8,128)} async-done(((f32[128,8,56]{2,1,0:T(8,128)}), f32[64,8,56]{2,1,0:T(8,128)}) %reduce-scatter.3.cloned.1.call-update) | async-done | bytes 114704 | tf_op jit(solution)/shard_map/reduce_scatter | solution.py:25
  284.8 41.0 %reduce-scatter.5.cloned.1.call-done = f32[8,8,56]{2,1,0:T(8,128)} async-done(((f32[64,8,56]{2,1,0:T(8,128)}), f32[8,8,56]{2,1,0:T(8,128)}) %reduce-scatter.5.cloned.1.call-update) | async-done | bytes 14352 | tf_op jit(solution)/shard_map/reduce_scatter | solution.py:25
  325.8 31.4 %all-reduce = f32[8,8,56]{2,1,0:T(8,128)} all-reduce(f32[8,8,56]{2,1,0:T(8,128)} %reduce-scatter.5.cloned.1.call-done), channel_id=4, replica_groups=mesh['grp'=2,'kvp_0'=8,'kvp_1'=2,'tp'=8] {'tp'}, use_global_device_ids=true, to_apply=%region_9.10.clone | all-reduce | flops 3584 | bytes 28672
  357.3 1.9 fusion.28
  (27 shorter events, 4.5 us)
Async XLA Ops:
  6.5 36.6 %copy-start = (bf16[8,384,576]{1,2,0:T(8,128)(2,1)S(1)}, bf16[8,384,576]{1,2,0:T(8,128)(2,1)}, u32[]{:S(2)}) copy-start(bf16[8,384,576]{1,2,0:T(8,128)(2,1)} %param.15) | copy-start | bytes 10616836
  43.8 0.7 copy-start.2
  45.9 9.8 %all-to-all-start = ((bf16[8,16,1]{0,2,1:T(2,128)(2,1)}), bf16[8,16,1]{0,2,1:T(2,128)(2,1)S(1)}, u32[]{:S(2)}, u32[]{:S(2)}) async-start(bf16[8,16,1]{0,2,1:T(2,128)(2,1)} %copy.24), calls=%async_computation | async-start | bytes 16384 | tf_op jit(solution)/shard_map/all_to_all | solution.py:94
  55.7 12.9 %all-to-all-start.1 = ((bf16[8,16,1,512]{3,0,2,1:T(8,128)(2,1)}), bf16[8,16,1,512]{3,0,2,1:T(8,128)(2,1)}, u32[]{:S(2)}, u32[]{:S(2)}) async-start(bf16[8,16,1,512]{3,0,2,1:T(8,128)(2,1)} %copy.27), calls=%async_computation.1 | async-start | bytes 262144 | tf_op jit(solution)/shard_map/all_to_all | solution.py:91
  61.1 197.2 %all-reduce.3.cloned.1.call-start = ((), (), s32[]{:S(2)}) async-start(), calls=%async_computation.4 | async-start | bytes 458752 | tf_op jit(solution)/shard_map/psum | solution.py:105
  72.5 211.7 %reduce-scatter.3.cloned.1.call-start = ((), (), s32[]{:S(2)}) async-start(), calls=%async_computation.5 | async-start | bytes 786432 | tf_op jit(solution)/shard_map/reduce_scatter | solution.py:25
  259.5 0.7 copy-start.1
  267.1 17.2 %copy-start.3 = (u32[256]{0:T(256)S(1)}, u32[256]{0:T(256)}, u32[]{:S(2)}) copy-start(u32[256]{0:T(256)} %constant.55) | copy-start | bytes 3076
  271.5 54.4 %reduce-scatter.5.cloned.1.call-start = ((), (), s32[]{:S(2)}) async-start(), calls=%async_computation.6 | async-start | bytes 294912 | tf_op jit(solution)/shard_map/reduce_scatter | solution.py:25
Sparse Core Ops, SparseCore 0:
  72.6 185.6 all-reduce.2
  271.6 12.5 reduce-scatter.2
  286.7 39.0 reduce-scatter.4
where the time goes:
time: 366 us
  waiting for transfers between devices  249 us (68%)
  blocking collectives  65.4 us (18%)
  matrix products  13.5 us (4%)
  between operations  13.2 us (4%)
  starting transfers between devices  9.14 us (2%)
  local copies, waits for them, and re-layouts  7.86 us (2%)
  other arithmetic  7.76 us (2%)
    psum x1, waiting for transfers between devices, per_device(): attn_whole = lax.psum(attention, KVP_TP)  186 us
    reduce_scatter x2, waiting for transfers between devices, sum_in_order(): blocks = lax.psum_scatter(blocks, axes[k], scatter_dimension=0, tiled=True)  53.6 us
    all_gather x1, blocking collectives, in_one_piece(): lax.all_gather(both, axis, axis=dim, tiled=True)  34 us
    unnamed x1, blocking collectives  31.4 us
  transfers between devices with their start and end apart: 5, of which 5 were waited for; matrix products, arithmetic and copies ran while one was open for 1% of the time, Pallas kernels for 0%

commit v1 on v0

--- a/solution.py
+++ b/solution.py
@@ -102,7 +102,7 @@
     model_width = norm_gain.shape[0]
     share_width = model_width // lax.axis_size(KVP_TP)
     share_start = lax.axis_index(KVP_TP) * share_width
-    attn_whole = lax.psum(attention, KVP_TP)
+    attn_whole = jnp.sum(lax.all_gather(attention, KVP_TP), axis=0)
     residual = hidden_in.astype(jnp.float32) + attn_whole
     mean_square = jnp.mean(residual * residual, axis=1)
     normed = (residual * lax.rsqrt(mean_square + 1e-06)[:, None] * norm_gain[None, :]).astype(

time: 366 us -> 317 us (0.87)
  waiting for transfers between devices: 249 us -> 192 us
  other arithmetic: 7.76 us -> 18 us
    psum x1 -> x0, waiting for transfers between devices: 186 us -> none  [per_device(): attn_whole = lax.psum(attention, KVP_TP)]
    all_gather x0 -> x1, waiting for transfers between devices: none -> 128 us  [per_device(): attn_whole = jnp.sum(lax.all_gather(attention, KVP_TP), axis=0)]
    reduce_sum x0 -> x1, other arithmetic: none -> 11.2 us  [per_device(): attn_whole = jnp.sum(lax.all_gather(attention, KVP_TP), axis=0)]
  transfers between devices with their start and end apart: 5 -> 5, of which waited for: 5 -> 5; matrix products, arithmetic and copies ran while one was open for 1% -> 2% of each run, Pallas kernels for 0% -> 0%
where the time goes in v1:
time: 317 us
  waiting for transfers between devices  192 us (61%)
  blocking collectives  65.4 us (21%)
  other arithmetic  18 us (6%)
  between operations  13.2 us (4%)
  matrix products  11.9 us (4%)
  starting transfers between devices  9.14 us (3%)
  local copies, waits for them, and re-layouts  7.87 us (2%)
    all_gather x1, waiting for transfers between devices, per_device(): attn_whole = jnp.sum(lax.all_gather(attention, KVP_TP), axis=0)  128 us
    reduce_scatter x2, waiting for transfers between devices, sum_in_order(): blocks = lax.psum_scatter(blocks, axes[k], scatter_dimension=0, tiled=True)  54.4 us
    all_gather x1, blocking collectives, in_one_piece(): lax.all_gather(both, axis, axis=dim, tiled=True)  34 us
    unnamed x1, blocking collectives  31.4 us
    reduce_sum x1, other arithmetic, per_device(): attn_whole = jnp.sum(lax.all_gather(attention, KVP_TP), axis=0)  11.2 us
  transfers between devices with their start and end apart: 5, of which 5 were waited for; matrix products, arithmetic and copies ran while one was open for 2% of the time, Pallas kernels for 0%

profile of v1, /device:TPU:514, one launch (start us, length us, event | category | flops | bytes accessed | tf_op | source)
XLA Modules:
  0.0 317.0 jit_solution(5335259182363710490)
XLA Ops:
  6.6 1.2 fusion.1
  7.7 0.7 pad_maximum_fusion
  8.4 34.0 %all_gather.9 = bf16[8,16,576]{2,0,1:T(8,128)(2,1)S(1)} all-gather(bf16[8,1,576]{2,0,1:T(8,128)(2,1)S(1)} %pad_maximum_fusion), channel_id=1, replica_groups=mesh['grp'=2,'kvp_0'=8,'kvp_1'=2,'tp'=8] {'kvp_0','kvp_1'}, dimensions={1}, use_global_device_ids=true | all-gather | bytes 156672 | tf_op jit(solution)/shard_map/all_gather | solution.py:13
  42.4 0.7 broadcast_compare_fusion
  43.8 0.7 copy-done.3
  45.9 3.6 %all-to-all-start = ((bf16[8,16,1]{0,2,1:T(2,128)(2,1)}), bf16[8,16,1]{0,2,1:T(2,128)(2,1)S(1)}, u32[]{:S(2)}, u32[]{:S(2)}) async-start(bf16[8,16,1]{0,2,1:T(2,128)(2,1)} %copy.18), calls=%async_computation | async-start | bytes 16384 | tf_op jit(solution)/shard_map/all_to_all | solution.py:94
  49.5 2.0 fusion.11
  51.6 0.7 copy.21
  52.3 3.4 %all-to-all-done = bf16[8,16,1]{0,2,1:T(2,128)(2,1)S(1)} async-done(((bf16[8,16,1]{0,2,1:T(2,128)(2,1)}), bf16[8,16,1]{0,2,1:T(2,128)(2,1)S(1)}, u32[]{:S(2)}, u32[]{:S(2)}) %all-to-all-start) | async-done | bytes 288 | tf_op jit(solution)/shard_map/all_to_all | solution.py:94
  55.7 5.4 %all-to-all-start.1 = ((bf16[8,16,1,512]{3,0,2,1:T(8,128)(2,1)}), bf16[8,16,1,512]{3,0,2,1:T(8,128)(2,1)}, u32[]{:S(2)}, u32[]{:S(2)}) async-start(bf16[8,16,1,512]{3,0,2,1:T(8,128)(2,1)} %copy.21), calls=%async_computation.1 | async-start | bytes 262144 | tf_op jit(solution)/shard_map/all_to_all | solution.py:91
  61.8 0.8 fusion.24
  62.8 5.9 %all-to-all-done.1 = bf16[8,16,1,512]{3,0,2,1:T(8,128)(2,1)} async-done(((bf16[8,16,1,512]{3,0,2,1:T(8,128)(2,1)}), bf16[8,16,1,512]{3,0,2,1:T(8,128)(2,1)}, u32[]{:S(2)}, u32[]{:S(2)}) %all-to-all-start.1) | async-done | bytes 131104 | tf_op jit(solution)/shard_map/all_to_all | solution.py:91
  68.7 1.0 multiply_reduce_fusion
  69.7 2.7 fusion.4
  72.5 127.6 %all-gather.3.cloned.1.call-done = f32[1024,7168]{1,0:T(8,128)} async-done(((f32[8,7168]{1,0:T(8,128)}), f32[1024,7168]{1,0:T(8,128)}) %all-gather.3.cloned.1.call-update) | async-done | bytes 29360144 | tf_op jit(solution)/shard_map/all_gather | solution.py:105
  200.2 11.2 %bitcast_reduce_fusion = f32[8,7168]{1,0:T(8,128)S(1)} fusion(f32[1024,7168]{1,0:T(8,128)} %all-gather.3.cloned.1.call-done), kind=kLoop, calls=%fused_computation | loop fusion | flops 7282688 | bytes 29589504 | tf_op jit(solution)/shard_map/reduce_sum | solution.py:105
  211.6 0.7 copy-done.1
  212.9 4.6 %fusion.3 = f32[8,7168]{1,0:T(8,128)} fusion(bf16[144,7168]{1,0:T(8,128)(2,1)} %param.23, bf16[7168,144]{0,1:T(8,128)(2,1)} %param.22, f32[8,144]{1,0:T(8,128)S(1)} %fusion.34, f32[8,7168]{1,0:T(8,128)} %copy-done.1, f32[7168]{0:T(1024)} %param.20, f32[8]{0:T(128)S(1)} %add_rsqrt_fusion), kind=kOutput, calls=%fused_computation.7 | convolution fusion | flops 33209088 | bytes 4620832 | tf_op jit(solution)/shard_map/dot_general | solution.py:115
  217.6 2.2 reshape.125
  219.8 2.2 copy.22
  222.1 13.4 %reduce-scatter.3.cloned.1.call-done = f32[64,8,56]{2,1,0:T(8,128)} async-done(((f32[128,8,56]{2,1,0:T(8,128)}), f32[64,8,56]{2,1,0:T(8,128)}) %reduce-scatter.3.cloned.1.call-update) | async-done | bytes 114704 | tf_op jit(solution)/shard_map/reduce_scatter | solution.py:25
  236.1 41.0 %reduce-scatter.5.cloned.1.call-done = f32[8,8,56]{2,1,0:T(8,128)} async-done(((f32[64,8,56]{2,1,0:T(8,128)}), f32[8,8,56]{2,1,0:T(8,128)}) %reduce-scatter.5.cloned.1.call-update) | async-done | bytes 14352 | tf_op jit(solution)/shard_map/reduce_scatter | solution.py:25
  277.1 31.4 %all-reduce = f32[8,8,56]{2,1,0:T(8,128)} all-reduce(f32[8,8,56]{2,1,0:T(8,128)} %reduce-scatter.5.cloned.1.call-done), channel_id=5, replica_groups=mesh['grp'=2,'kvp_0'=8,'kvp_1'=2,'tp'=8] {'tp'}, use_global_device_ids=true, to_apply=%region_9.10.clone | all-reduce | flops 3584 | bytes 28672
  308.5 1.9 fusion.28
  (34 shorter events, 4.7 us)
Async XLA Ops:
  6.5 36.6 %copy-start = (bf16[8,384,576]{1,2,0:T(8,128)(2,1)S(1)}, bf16[8,384,576]{1,2,0:T(8,128)(2,1)}, u32[]{:S(2)}) copy-start(bf16[8,384,576]{1,2,0:T(8,128)(2,1)} %param.15) | copy-start | bytes 10616836
  43.8 0.7 copy-start.3
  45.9 9.8 %all-to-all-start = ((bf16[8,16,1]{0,2,1:T(2,128)(2,1)}), bf16[8,16,1]{0,2,1:T(2,128)(2,1)S(1)}, u32[]{:S(2)}, u32[]{:S(2)}) async-start(bf16[8,16,1]{0,2,1:T(2,128)(2,1)} %copy.18), calls=%async_computation | async-start | bytes 16384 | tf_op jit(solution)/shard_map/all_to_all | solution.py:94
  55.7 12.9 %all-to-all-start.1 = ((bf16[8,16,1,512]{3,0,2,1:T(8,128)(2,1)}), bf16[8,16,1,512]{3,0,2,1:T(8,128)(2,1)}, u32[]{:S(2)}, u32[]{:S(2)}) async-start(bf16[8,16,1,512]{3,0,2,1:T(8,128)(2,1)} %copy.21), calls=%async_computation.1 | async-start | bytes 262144 | tf_op jit(solution)/shard_map/all_to_all | solution.py:91
  61.1 139.1 %all-gather.3.cloned.1.call-start = ((), (), s32[]{:S(2)}) async-start(), calls=%async_computation.6 | async-start | bytes 29589504 | tf_op jit(solution)/shard_map/all_gather | solution.py:105
  72.5 163.0 %reduce-scatter.3.cloned.1.call-start = ((), (), s32[]{:S(2)}) async-start(), calls=%async_computation.4 | async-start | bytes 786432 | tf_op jit(solution)/shard_map/reduce_scatter | solution.py:25
  200.2 11.2 %copy-start.4 = (bf16[8,7168]{1,0:T(8,128)(2,1)S(1)}, bf16[8,7168]{1,0:T(8,128)(2,1)}, u32[]{:S(2)}) copy-start(bf16[8,7168]{1,0:T(8,128)(2,1)} %param.12) | copy-start | bytes 344068
  200.2 12.1 %copy-start.2 = (bf16[7168,144]{0,1:T(8,128)(2,1)S(1)}, bf16[7168,144]{0,1:T(8,128)(2,1)}, u32[]{:S(2)}) copy-start(bf16[7168,144]{0,1:T(8,128)(2,1)} %param.21) | copy-start | bytes 6193156
  200.2 12.1 %copy-start.5 = (f32[7168]{0:T(1024)S(1)}, f32[7168]{0:T(1024)}, u32[]{:S(2)}) copy-start(f32[7168]{0:T(1024)} %param.20) | copy-start | bytes 86020
  211.6 0.7 copy-start.1
  217.6 18.0 %copy-start.6 = (u32[256]{0:T(256)S(1)}, u32[256]{0:T(256)}, u32[]{:S(2)}) copy-start(u32[256]{0:T(256)} %constant.55) | copy-start | bytes 3076
  222.0 55.1 %reduce-scatter.5.cloned.1.call-start = ((), (), s32[]{:S(2)}) async-start(), calls=%async_computation.5 | async-start | bytes 294912 | tf_op jit(solution)/shard_map/reduce_scatter | solution.py:25
Sparse Core Ops, SparseCore 0:
  72.6 127.5 all-gather.2
  222.1 13.3 reduce-scatter.2
  238.0 39.0 reduce-scatter.4
